TPU v7x, 256 devices: a whole 4x4x8 slice. The times are simulated.
256 devices in a mesh: unit: 4 (over y), bank: 4 (over x), zero: 16 (over z, core).
Axes of the slice: x: 4, y: 4, z: 8, core: 2. Of those that a mesh axis runs over, the one named last changes fastest.
Arguments:
- train_down: float32 [256, 1024, 2048], P(('unit', 'bank'), None, 'zero'), parts along dimension 0, may hold values from -0.25 to 0.25
- router_weight: float32 [8192, 64], P(('unit', 'zero'), 'bank'), parts along dimension 0, may hold values from -0.125 to 0.125
- router_gain: float32 [8192], P(('unit', 'zero')), parts along dimension 0, may hold values from 0.25 to 1.75
Outputs:
- ready_down: bfloat16 [256, 1024, 2048], P(('unit', 'bank'), 'zero'), parts along dimension 0
- scale_down: float32 [256, 1024], P(('unit', 'bank'), 'zero'), parts along dimension 0
- serve_router: bfloat16 [8192, 64], P('unit'), parts along dimension 0
There are 4 independent parts, one for each index of `unit`. A program takes and returns all parts, laid end to end along the dimension named above; each array names one. Nothing has to cross between parts.
All inputs are finite; a program needn't handle non-finite values.
Results may differ from a plain program's by a relative error of at most 0.001.
Values may be sent and summed in bfloat16 or wider, within the bound.
A program may use at most 128 MiB of HBM per device.

v0:
```python
import jax
import jax.numpy as jnp
from jax import lax
from jax.sharding import Mesh
from jax.sharding import PartitionSpec as P

ZERO = ("zero_0", "zero_1")
UNIT_ZERO = ("unit", "zero_0", "zero_1")


def gathered_total(value, axis):
    tiles = lax.all_gather(value, axis)
    return tiles.max(axis=0)


def in_blocks(value, dim, length):
    return jnp.stack(jnp.split(value, length, axis=dim))


def joined_along(tiles, dim):
    tiles = jnp.moveaxis(tiles, 0, dim)
    dims = tiles.shape
    return tiles.reshape(*dims[:dim], dims[dim] * dims[dim + 1], *dims[dim + 2 :])


def turned_blocks(tiles, axes, sequence):
    dims = [lax.axis_size(a) for a in axes]
    tiles = tiles.reshape(*dims, *tiles.shape[1:])
    for k in sequence:
        tiles = lax.all_to_all(tiles, axes[k], split_axis=k, concat_axis=k, tiled=True)
    return tiles.reshape(-1, *tiles.shape[len(axes) :])


def two_step_exchange(value, groups, sequence, split_dim, concat_dim):
    length = lax.axis_size(groups[0]) * lax.axis_size(groups[1])
    tiles = in_blocks(value, split_dim, length)
    return joined_along(turned_blocks(tiles, groups, sequence), concat_dim)


def per_device(train_down, router_weight, router_gain):
    scale_down = gathered_total(jnp.max(jnp.abs(train_down), axis=2), ZERO)
    narrow_down = (train_down / jnp.expand_dims(scale_down, 2)).astype(jnp.bfloat16)
    ready_down = two_step_exchange(narrow_down, ("zero_0", "zero_1"), (1, 0), 1, 2)
    scale_down = lax.dynamic_slice_in_dim(
        scale_down, lax.axis_index(ZERO) * ready_down.shape[1], ready_down.shape[1], axis=1
    )
    part_router = (router_weight * router_gain[:, None]).astype(jnp.bfloat16)
    row_router = lax.all_gather(part_router, ZERO, axis=0, tiled=True)
    serve_router = lax.all_gather(row_router, "bank", axis=1, tiled=True)
    return (ready_down, scale_down, serve_router)


def solution(mesh):
    torus = Mesh(
        mesh.devices.reshape(mesh.shape["unit"], mesh.shape["bank"], 8, 2),
        ("unit", "bank", "zero_0", "zero_1"),
    )
    placed = (P(("unit", "bank"), None, ZERO), P(UNIT_ZERO, "bank"), P(UNIT_ZERO))
    return jax.shard_map(
        per_device,
        mesh=torus,
        in_specs=placed,
        out_specs=(P(("unit", "bank"), ZERO, None), P(("unit", "bank"), ZERO), P("unit", None)),
        check_vma=False,
    )
```

profile of v0, /device:TPU:2, one launch (start us, length us, event | category | flops | bytes accessed | tf_op | source)
XLA Modules:
  0.0 208.9 jit_solution(14406718394577058157)
XLA Ops:
  7.2 0.0 all-gather.3.cloned.1.call-start
  7.2 6.2 %abs_reduce_fusion = f32[16,1024]{1,0:T(8,128)} fusion(f32[16,1024,128]{2,1,0:T(8,128)} %param.3), kind=kLoop, calls=%fused_computation.1 | loop fusion | flops 4177920 | bytes 8454144 | tf_op jit(solution)/shard_map/reduce_max | solution.py:41
  13.5 0.0 all-gather.3.cloned.1.call-update
  13.5 41.7 %all-gather.3.cloned.1.call-done = f32[256,1024]{1,0:T(8,128)} async-done(((f32[16,1024]{1,0:T(8,128)}), f32[256,1024]{1,0:T(8,128)}) %all-gather.3.cloned.1.call-update) | async-done | bytes 1048592 | tf_op jit(solution)/shard_map/all_gather | solution.py:12
  55.1 1.3 reduce_max.19
  56.4 5.3 %divide_convert_fusion = bf16[16,1024,128]{2,1,0:T(8,128)(2,1)S(1)} fusion(f32[16,1024,128]{2,1,0:T(8,128)} %param.3, f32[16,1024]{1,0:T(8,128)S(1)} %reduce_max.19), kind=kLoop, calls=%fused_computation | loop fusion | flops 4194304 | bytes 12648448 | tf_op jit(solution)/shard_map/convert_element_type | solution.py:42
  62.4 1.3 copy.12
  63.7 7.1 %all_to_all.10 = bf16[8,2,16,64,128]{4,3,2,0,1:T(8,128)(2,1)S(1)} all-to-all(bf16[8,2,16,64,128]{4,3,2,0,1:T(8,128)(2,1)S(1)} %copy.12), channel_id=1, replica_groups=mesh['unit'=4,'bank'=4,'zero_0'=8,'zero_1'=2] {'zero_1'}, dimensions={1} | all-to-all | bytes 8388608 | tf_op jit(solution)/shard_map/all_to_all | solution.py:30
  70.8 3.0 %copy.13 = bf16[8,2,16,64,128]{4,3,2,1,0:T(8,128)(2,1)} copy(bf16[8,2,16,64,128]{4,3,2,0,1:T(8,128)(2,1)S(1)} %all_to_all.10) | data formatting | bytes 8388608 | tf_op jit(solution)/shard_map/all_to_all | solution.py:30
  73.8 0.0 copy-start
  73.8 0.0 copy-start.1
  73.8 4.7 %all-to-all-start.1 = ((bf16[8,2,16,64,128]{4,3,2,1,0:T(8,128)(2,1)}), bf16[8,2,16,64,128]{4,3,2,1,0:T(8,128)(2,1)}, u32[]{:S(2)}, u32[]{:S(2)}) async-start(bf16[8,2,16,64,128]{4,3,2,1,0:T(8,128)(2,1)} %copy.13), calls=%async_computation.1 | async-start | bytes 8388608 | tf_op jit(solution)/shard_map/all_to_all | solution.py:30
  78.5 0.0 copy-done
  78.5 0.0 copy-done.1
  78.5 104.4 %all_gather.14 = bf16[2048,16]{0,1:T(8,128)(2,1)S(1)} all-gather(bf16[128,16]{0,1:T(8,128)(2,1)S(1)} %multiply_convert_fusion), channel_id=1, replica_groups=mesh['unit'=4,'bank'=4,'zero_0'=8,'zero_1'=2] {'zero_0','zero_1'}, dimensions={0}, use_global_device_ids=true | all-gather | bytes 69632 | tf_op jit(solution)/shard_map/all_gather | solution.py:48
  182.9 12.5 %all_gather.15 = bf16[2048,64]{0,1:T(8,128)(2,1)S(1)} all-gather(bf16[2048,16]{0,1:T(8,128)(2,1)S(1)} %all_gather.14), channel_id=1, replica_groups=mesh['unit'=4,'bank'=4,'zero_0'=8,'zero_1'=2] {'bank'}, dimensions={1}, use_global_device_ids=true | all-gather | bytes 327680 | tf_op jit(solution)/shard_map/all_gather | solution.py:49
  195.4 0.7 constant_dynamic-slice_fusion
  196.0 0.0 all-to-all-done.1
  196.0 5.3 %copy.17 = bf16[16,16,8,8,128]{4,3,0,2,1:T(8,128)(2,1)} copy(bf16[16,16,8,8,128]{4,3,2,1,0:T(8,128)(2,1)} %bitcast.21) | data formatting | bytes 8388608 | tf_op jit(solution)/shard_map/reshape | solution.py:23
  201.4 0.7 copy.34
  (17 shorter events, 0.6 us)
Async XLA Ops:
  7.2 48.0 %all-gather.3.cloned.1.call-start = ((), (), s32[]{:S(2)}) async-start(), calls=%async_computation.2 | async-start | bytes 1114112 | tf_op jit(solution)/shard_map/all_gather | solution.py:12
  73.8 4.7 %copy-start = (f32[128,16]{0,1:T(8,128)S(1)}, f32[128,16]{0,1:T(8,128)}, u32[]{:S(2)}) copy-start(f32[128,16]{0,1:T(8,128)} %param.4) | copy-start | bytes 24580
  73.8 4.7 %copy-start.1 = (f32[128]{0:T(128)S(1)}, f32[128]{0:T(128)}, u32[]{:S(2)}) copy-start(f32[128]{0:T(128)} %param.5) | copy-start | bytes 1540
  73.8 122.2 %all-to-all-start.1 = ((bf16[8,2,16,64,128]{4,3,2,1,0:T(8,128)(2,1)}), bf16[8,2,16,64,128]{4,3,2,1,0:T(8,128)(2,1)}, u32[]{:S(2)}, u32[]{:S(2)}) async-start(bf16[8,2,16,64,128]{4,3,2,1,0:T(8,128)(2,1)} %copy.13), calls=%async_computation.1 | async-start | bytes 8388608 | tf_op jit(solution)/shard_map/all_to_all | solution.py:30
Sparse Core Ops, SparseCore 0:
  13.6 41.4 all-gather.2
where the time goes:
time: 209 us
  blocking collectives  124 us (59%)
  waiting for transfers between devices  41.7 us (20%)
  between operations  14.2 us (7%)
  other arithmetic  12.8 us (6%)
  local copies, waits for them, and re-layouts  11.6 us (6%)
  starting transfers between devices  4.71 us (2%)
    all_gather x1, blocking collectives, per_device(): row_router = lax.all_gather(part_router, ZERO, axis=0, tiled=True)  104 us
    all_gather x1, waiting for transfers between devices, gathered_total(): tiles = lax.all_gather(value, axis)  41.7 us
    all_gather x1, blocking collectives, per_device(): serve_router = lax.all_gather(row_router, 'bank', axis=1, tiled=True)  12.5 us
    all_to_all x1, blocking collectives, turned_blocks(): lax.all_to_all(tiles, axes[k], split_axis=k, concat_axis=k, tiled=True)  7.1 us
    reduce_max x1, other arithmetic, per_device(): scale_down = gathered_total(jnp.max(jnp.abs(train_down), axis=2), ZERO)  6.25 us
    reshape x1, local copies, waits for them, and re-layouts, joined_along(): tiles.reshape(*dims[:dim], dims[dim] * dims[dim + 1], *dims[dim + 2:])  5.35 us
    convert_element_type x1, other arithmetic, per_device(): (train_down / jnp.expand_dims(scale_down, 2)).astype(jnp.bfloat16)  5.26 us
    all_to_all x1, starting transfers between devices, turned_blocks(): lax.all_to_all(tiles, axes[k], split_axis=k, concat_axis=k, tiled=True)  4.67 us
  transfers between devices with their start and end apart: 2, of which 1 were waited for; matrix products, arithmetic and copies ran while one was open for 0% of the time, Pallas kernels for 0%

commit v1 on v0

--- a/solution.py
+++ b/solution.py
@@ -3,6 +3,7 @@
 from jax import lax
 from jax.sharding import Mesh
 from jax.sharding import PartitionSpec as P
+from jax.lax import all_to_all, axis_size
 
 ZERO = ("zero_0", "zero_1")
 UNIT_ZERO = ("unit", "zero_0", "zero_1")
@@ -46,7 +47,10 @@
     )
     part_router = (router_weight * router_gain[:, None]).astype(jnp.bfloat16)
     row_router = lax.all_gather(part_router, ZERO, axis=0, tiled=True)
-    serve_router = lax.all_gather(row_router, "bank", axis=1, tiled=True)
+    _list_paths = lambda piece_in: jnp.concatenate(
+        all_to_all(jnp.stack([piece_in for _ in range(axis_size("bank"))], 0), "bank", 0, 0), 1
+    )
+    serve_router = _list_paths(row_router)
     return (ready_down, scale_down, serve_router)
 
 

time: 209 us -> 198 us (0.947)
  blocking collectives: 124 us -> 28.3 us
  waiting for transfers between devices: 41.7 us -> 117 us
  starting transfers between devices: 4.71 us -> 9.39 us
  local copies, waits for them, and re-layouts: 11.6 us -> 14.8 us
    all_to_all x1, waiting for transfers between devices: 0.01 us -> 95.6 us  [turned_blocks(): lax.all_to_all(tiles, axes[k], split_axis=k, concat_axis=k, tiled=True)]
    all_gather x1, blocking collectives: 104 us -> 20.1 us  [per_device(): row_router = lax.all_gather(part_router, ZERO, axis=0, tiled=True)]
    all_gather x1, waiting for transfers between devices: 41.7 us -> 21.5 us  [gathered_total(): tiles = lax.all_gather(value, axis)]
    all_gather x1 -> x0, blocking collectives: 12.5 us -> none  [per_device(): serve_router = lax.all_gather(row_router, 'bank', axis=1, tiled=True)]
    all_to_all x0 -> x1, starting transfers between devices: none -> 4.8 us  [per_device(): all_to_all(jnp.stack([piece_in for _ in range(axis_size('bank'))], 0), 'b...]
    all_to_all x1, local copies, waits for them, and re-layouts: 2.97 us -> 5.52 us  [turned_blocks(): lax.all_to_all(tiles, axes[k], split_axis=k, concat_axis=k, tiled=True)]
  transfers between devices with their start and end apart: 2 -> 3, of which waited for: 1 -> 2; matrix products, arithmetic and copies ran while one was open for 0% -> 3% of each run, Pallas kernels for 0% -> 0%
where the time goes in v1:
time: 198 us; the launch traced here: 197 us
  waiting for transfers between devices  117 us (59%)
  blocking collectives  28.3 us (14%)
  local copies, waits for them, and re-layouts  14.8 us (7%)
  between operations  14.2 us (7%)
  other arithmetic  12.8 us (6%)
  starting transfers between devices  9.39 us (5%)
    all_to_all x1, waiting for transfers between devices, turned_blocks(): lax.all_to_all(tiles, axes[k], split_axis=k, concat_axis=k, tiled=True)  95.6 us
    all_gather x1, waiting for transfers between devices, gathered_total(): tiles = lax.all_gather(value, axis)  21.5 us
    all_gather x1, blocking collectives, per_device(): row_router = lax.all_gather(part_router, ZERO, axis=0, tiled=True)  20.1 us
    all_to_all x1, blocking collectives, turned_blocks(): lax.all_to_all(tiles, axes[k], split_axis=k, concat_axis=k, tiled=True)  8.15 us
    reduce_max x1, other arithmetic, per_device(): scale_down = gathered_total(jnp.max(jnp.abs(train_down), axis=2), ZERO)  6.25 us
    all_to_all x1, local copies, waits for them, and re-layouts, turned_blocks(): lax.all_to_all(tiles, axes[k], split_axis=k, concat_axis=k, tiled=True)  5.52 us
    reshape x1, local copies, waits for them, and re-layouts, joined_along(): tiles.reshape(*dims[:dim], dims[dim] * dims[dim + 1], *dims[dim + 2:])  5.35 us
    convert_element_type x1, other arithmetic, per_device(): (train_down / jnp.expand_dims(scale_down, 2)).astype(jnp.bfloat16)  5.26 us
  transfers between devices with their start and end apart: 3, of which 2 were waited for; matrix products, arithmetic and copies ran while one was open for 3% of the time, Pallas kernels for 0%

profile of v1, /device:TPU:2, one launch (start us, length us, event | category | flops | bytes accessed | tf_op | source)
XLA Modules:
  0.0 196.6 jit_solution(3755257042915347789)
XLA Ops:
  7.2 0.0 copy-start
  7.2 0.0 copy-start.1
  7.2 0.0 all-gather.3.cloned.1.call-start
  7.2 6.2 %abs_reduce_fusion = f32[16,1024]{1,0:T(8,128)} fusion(f32[16,1024,128]{2,1,0:T(8,128)} %param.3), kind=kLoop, calls=%fused_computation.1 | loop fusion | flops 4177920 | bytes 8454144 | tf_op jit(solution)/shard_map/reduce_max | solution.py:42
  13.5 0.0 all-gather.3.cloned.1.call-update
  13.5 0.0 copy-done
  13.5 0.0 copy-done.1
  13.5 20.1 %all_gather.11 = bf16[2048,16]{0,1:T(8,128)(2,1)S(1)} all-gather(bf16[128,16]{0,1:T(8,128)(2,1)S(1)} %multiply_convert_fusion), channel_id=1, replica_groups=mesh['unit'=4,'bank'=4,'zero_0'=8,'zero_1'=2] {'zero_0','zero_1'}, dimensions={0}, use_global_device_ids=true | all-gather | bytes 69632 | tf_op jit(solution)/shard_map/all_gather | solution.py:49
  33.7 21.5 %all-gather.3.cloned.1.call-done = f32[256,1024]{1,0:T(8,128)} async-done(((f32[16,1024]{1,0:T(8,128)}), f32[256,1024]{1,0:T(8,128)}) %all-gather.3.cloned.1.call-update) | async-done | bytes 1048592 | tf_op jit(solution)/shard_map/all_gather | solution.py:13
  55.2 1.3 reduce_max.19
  56.5 5.3 %divide_convert_fusion = bf16[16,1024,128]{2,1,0:T(8,128)(2,1)S(1)} fusion(f32[16,1024,128]{2,1,0:T(8,128)} %param.3, f32[16,1024]{1,0:T(8,128)S(1)} %reduce_max.19), kind=kLoop, calls=%fused_computation | loop fusion | flops 4194304 | bytes 12648448 | tf_op jit(solution)/shard_map/convert_element_type | solution.py:43
  62.4 1.3 copy.12
  63.7 8.2 %all_to_all.15 = bf16[8,2,16,64,128]{4,3,2,0,1:T(8,128)(2,1)} all-to-all(bf16[8,2,16,64,128]{4,3,2,0,1:T(8,128)(2,1)S(1)} %copy.12), channel_id=1, replica_groups=mesh['unit'=4,'bank'=4,'zero_0'=8,'zero_1'=2] {'zero_1'}, dimensions={1} | all-to-all | bytes 8388608 | tf_op jit(solution)/shard_map/all_to_all | solution.py:31
  71.9 0.7 stack.75
  72.6 4.8 %all-to-all-start.2 = ((bf16[4,2048,16]{1,2,0:T(8,128)(2,1)}), bf16[4,2048,16]{1,2,0:T(8,128)(2,1)S(1)}, u32[]{:S(2)}, u32[]{:S(2)}) async-start(bf16[4,2048,16]{1,2,0:T(8,128)(2,1)} %stack.75), calls=%async_computation.2 | async-start | bytes 524288 | tf_op jit(solution)/shard_map/all_to_all | solution.py:51
  77.4 5.5 %copy.13 = bf16[8,2,16,64,128]{4,3,2,1,0:T(8,128)(2,1)} copy(bf16[8,2,16,64,128]{4,3,2,0,1:T(8,128)(2,1)} %all_to_all.15) | data formatting | bytes 8388608 | tf_op jit(solution)/shard_map/all_to_all | solution.py:31
  82.9 0.0 all-to-all-done.2
  82.9 4.5 %all-to-all-start.1 = ((bf16[8,2,16,64,128]{4,3,2,1,0:T(8,128)(2,1)}), bf16[8,2,16,64,128]{4,3,2,1,0:T(8,128)(2,1)}, u32[]{:S(2)}, u32[]{:S(2)}) async-start(bf16[8,2,16,64,128]{4,3,2,1,0:T(8,128)(2,1)} %copy.13), calls=%async_computation.1 | async-start | bytes 8388608 | tf_op jit(solution)/shard_map/all_to_all | solution.py:31
  87.5 0.7 constant_dynamic-slice_fusion
  88.2 95.6 %all-to-all-done.1 = bf16[8,2,16,64,128]{4,3,2,1,0:T(8,128)(2,1)} async-done(((bf16[8,2,16,64,128]{4,3,2,1,0:T(8,128)(2,1)}), bf16[8,2,16,64,128]{4,3,2,1,0:T(8,128)(2,1)}, u32[]{:S(2)}, u32[]{:S(2)}) %all-to-all-start.1) | async-done | bytes 4194336 | tf_op jit(solution)/shard_map/all_to_all | solution.py:31
  183.7 5.3 %copy.17 = bf16[16,16,8,8,128]{4,3,0,2,1:T(8,128)(2,1)} copy(bf16[16,16,8,8,128]{4,3,2,1,0:T(8,128)(2,1)} %bitcast.24) | data formatting | bytes 8388608 | tf_op jit(solution)/shard_map/reshape | solution.py:24
  189.1 0.7 copy.34
  (17 shorter events, 0.6 us)
Async XLA Ops:
  7.2 6.3 %copy-start = (f32[128,16]{0,1:T(8,128)S(1)}, f32[128,16]{0,1:T(8,128)}, u32[]{:S(2)}) copy-start(f32[128,16]{0,1:T(8,128)} %param.4) | copy-start | bytes 24580
  7.2 6.3 %copy-start.1 = (f32[128]{0:T(128)S(1)}, f32[128]{0:T(128)}, u32[]{:S(2)}) copy-start(f32[128]{0:T(128)} %param.5) | copy-start | bytes 1540
  7.2 48.0 %all-gather.3.cloned.1.call-start = ((), (), s32[]{:S(2)}) async-start(), calls=%async_computation.3 | async-start | bytes 1114112 | tf_op jit(solution)/shard_map/all_gather | solution.py:13
  72.6 10.3 %all-to-all-start.2 = ((bf16[4,2048,16]{1,2,0:T(8,128)(2,1)}), bf16[4,2048,16]{1,2,0:T(8,128)(2,1)S(1)}, u32[]{:S(2)}, u32[]{:S(2)}) async-start(bf16[4,2048,16]{1,2,0:T(8,128)(2,1)} %stack.75), calls=%async_computation.2 | async-start | bytes 524288 | tf_op jit(solution)/shard_map/all_to_all | solution.py:51
  82.9 100.8 %all-to-all-start.1 = ((bf16[8,2,16,64,128]{4,3,2,1,0:T(8,128)(2,1)}), bf16[8,2,16,64,128]{4,3,2,1,0:T(8,128)(2,1)}, u32[]{:S(2)}, u32[]{:S(2)}) async-start(bf16[8,2,16,64,128]{4,3,2,1,0:T(8,128)(2,1)} %copy.13), calls=%async_computation.1 | async-start | bytes 8388608 | tf_op jit(solution)/shard_map/all_to_all | solution.py:31
Sparse Core Ops, SparseCore 0:
  13.6 41.4 all-gather.2
